TPU v7x, 32 devices: a whole 2x2x4 slice. The times are simulated.
32 devices in a mesh: face: 8 (over z, core), sub: 4 (over y, x).
Axes of the slice: x: 2, y: 2, z: 4, core: 2. Of those that a mesh axis runs over, the one named last changes fastest.
Arguments:
- mesh_latent: bfloat16 [8192, 512], P(('face', 'sub')), may hold values from -6 to 6
- edge_latent: bfloat16 [65536, 512], P(('face', 'sub')), may hold values from -6 to 6
- grid_features: bfloat16 [8192, 384], P(('face', 'sub')), may hold values from -6 to 6
- senders: int32 [65536], P(('face', 'sub')), may hold values from 0 to 383, as said below
- receivers: int32 [65536], P(('face', 'sub')), may hold values from 0 to 255
- send_lists: int32 [32, 4, 32], P(('face', 'sub')), may hold values from -1 to 255, as said below
- link_sources: int32 [16384], P(('face', 'sub')), may hold values from 0 to 255
- link_targets: int32 [16384], P(('face', 'sub')), may hold values from 0 to 255
- node_area: float32 [8192], P(('face', 'sub')), may hold values from 0.25 to 4.5
- grid_weight: bfloat16 [384, 512], P(None, 'sub'), may hold values from -0.3125 to 0.3125
- encode_weight: bfloat16 [1024, 512], P('sub'), may hold values from -0.1875 to 0.1875
- edge_first: bfloat16 [1, 1536, 512], P(None, 'sub'), may hold values from -0.15625 to 0.15625
- edge_second: bfloat16 [1, 512, 512], P(None, 'sub'), may hold values from -0.25 to 0.25
- node_first: bfloat16 [1, 1024, 512], P(None, 'sub'), may hold values from -0.1875 to 0.1875
- node_second: bfloat16 [1, 512, 512], P(None, 'sub'), may hold values from -0.25 to 0.25
Outputs:
- mesh_result: bfloat16 [8192, 512], P(('face', 'sub'))
- edge_result: bfloat16 [65536, 512], P(('face', 'sub'))
- masses: float32 [1, 512], replicated
Inputs may be any that keep to these rules, and one draw needn't show every extreme that they name: `send_lists`: entries are the sending partition's own node numbers, or -1 for an unused slot; in every list the used slots come first, hold distinct nodes and number 32 // 2 or more; for every list number some partition uses all 32 slots. `senders`: A value below 256 names one of the partition's own nodes; 256 + d * 32 + k names slot k of the list with number d that the partition receives, and that slot is always a used one.
All inputs are finite; a program needn't handle non-finite values.
Results may differ from a plain program's by a relative error of at most 0.008.
Values may be sent and summed in bfloat16 or wider, within the bound.
A program may use at most 64 MiB of HBM per device.

v0:
```python
import jax
import jax.numpy as jnp
from jax import lax
from jax.sharding import PartitionSpec as P


def passed_along(value, axis, steps):
    count = lax.axis_size(axis)
    pairs = [(source, (source + steps) % count) for source in range(count)]
    return lax.ppermute(value, axis, pairs)


def fold_rows(weight, operand):
    return jnp.dot(
        operand,
        lax.all_gather(weight, "sub", axis=0, tiled=True),
        preferred_element_type=jnp.float32,
    )


def edge_rows(weight, operand):
    storage = jnp.zeros((1, weight.shape[1]), jnp.bfloat16)
    total = jnp.dot(
        operand,
        lax.all_gather(weight, "sub", axis=0, tiled=True),
        preferred_element_type=jnp.float32,
    )
    return (total, storage)


def along_face(values, offset):
    return passed_along(values, "face", offset)


def along_sub(values, offset):
    return passed_along(values, "sub", offset)


def per_device(
    mesh_latent,
    edge_latent,
    grid_features,
    senders,
    receivers,
    send_lists,
    link_sources,
    link_targets,
    node_area,
    grid_weight,
    encode_weight,
    edge_first,
    edge_second,
    node_first,
    node_second,
):
    node_rows = mesh_latent.shape[0]
    nodes_all = node_rows * lax.axis_size("face") * lax.axis_size("sub")
    grid_latent = jax.nn.silu(
        jnp.dot(
            grid_features,
            lax.all_gather(grid_weight, "sub", axis=1, tiled=True),
            preferred_element_type=jnp.float32,
        )
    ).astype(jnp.bfloat16)

    def project(weight, operand):
        return fold_rows(weight, operand)

    node_ids = jnp.arange(node_rows, dtype=jnp.int32)
    joined = jnp.concatenate(
        [jnp.take(grid_latent, link_sources, axis=0), jnp.take(mesh_latent, link_targets, axis=0)],
        axis=1,
    )
    messages = jax.nn.silu(project(encode_weight, joined)).astype(jnp.bfloat16)
    target_onehot = (link_targets[:, None] == node_ids[None, :]).astype(jnp.bfloat16)
    arriving = lax.dot_general(
        target_onehot, messages, (((0,), (0,)), ((), ())), preferred_element_type=jnp.float32
    )
    latent = (mesh_latent.astype(jnp.float32) + arriving).astype(jnp.bfloat16)
    halo_lists = send_lists[0]
    list_mask = (halo_lists >= 0)[:, :, None]
    receive_onehot = (receivers[:, None] == node_ids[None, :]).astype(jnp.bfloat16)
    edge_state = edge_latent
    picked = jnp.take(latent, jnp.maximum(halo_lists, 0), axis=0)
    picked = jnp.where(list_mask, picked, jnp.zeros((), jnp.bfloat16))
    lower_face = along_face(picked[0], 1)
    upper_face = along_face(picked[1], -1)
    lower_sub = along_sub(picked[2], 1)
    upper_sub = along_sub(picked[3], -1)
    arrived = jnp.concatenate([lower_face, upper_face, lower_sub, upper_sub], axis=0)
    receiving_rows = jnp.take(latent, receivers, axis=0)
    node_table = jnp.concatenate([latent, arrived], axis=0)
    inputs = jnp.concatenate(
        [edge_state, jnp.take(node_table, senders, axis=0), receiving_rows], axis=1
    )
    before, unused_rows = edge_rows(edge_first[0], inputs)
    hidden = jax.nn.silu(before).astype(jnp.bfloat16)
    edge_state = (edge_state.astype(jnp.float32) + project(edge_second[0], hidden)).astype(
        jnp.bfloat16
    )
    incoming = lax.dot_general(
        receive_onehot, edge_state, (((0,), (0,)), ((), ())), preferred_element_type=jnp.float32
    ).astype(jnp.bfloat16)
    node_hidden = jax.nn.silu(
        project(node_first[0], jnp.concatenate([latent, incoming], axis=1))
    ).astype(jnp.bfloat16)
    latent = (latent.astype(jnp.float32) + project(node_second[0], node_hidden)).astype(
        jnp.bfloat16
    )
    totals = [jnp.dot(node_area, latent.astype(jnp.float32), precision=lax.Precision.HIGHEST)]
    stacked = lax.psum(jnp.stack(totals), ("face", "sub"))
    masses = stacked / nodes_all
    return (latent, edge_state, masses)


def solution(mesh):
    in_specs = (
        P(("face", "sub"), None),
        P(("face", "sub"), None),
        P(("face", "sub"), None),
        P(("face", "sub")),
        P(("face", "sub")),
        P(("face", "sub"), None, None),
        P(("face", "sub")),
        P(("face", "sub")),
        P(("face", "sub")),
        P(None, "sub"),
        P("sub", None),
        P(None, "sub", None),
        P(None, "sub", None),
        P(None, "sub", None),
        P(None, "sub", None),
    )
    out_specs = (P(("face", "sub"), None), P(("face", "sub"), None), P())
    return jax.shard_map(
        per_device, mesh=mesh, in_specs=in_specs, out_specs=out_specs, check_vma=False
    )
```

profile of v0, /device:TPU:0, one launch (start us, length us, event | category | flops | bytes accessed | tf_op | source)
XLA Modules:
  0.0 153.9 jit_solution(15797503033091889898)
XLA Ops:
  7.2 0.0 copy-start
  7.2 0.0 all-gather.8.cloned.1.call-start
  7.2 0.7 all-gather.8.cloned.1.call-update
  7.9 0.0 all-gather.10.cloned.1.call-start
  8.0 0.7 all-gather.10.cloned.1.call-update
  8.7 0.0 all-gather.12.cloned.1.call-start
  8.7 0.7 all-gather.12.cloned.1.call-update
  9.4 0.7 compare_select_fusion.2
  10.1 0.7 compare_and_fusion.2
  10.8 0.7 compare_select_fusion.3
  11.5 0.7 compare_and_fusion.3
  12.2 0.7 broadcast_maximum_fusion
  12.8 0.7 compare_bitcast_fusion.1
  13.5 0.7 fusion.46
  14.2 1.3 compare_and_fusion.1
  15.5 0.7 fusion.47
  16.2 1.3 compare_and_fusion
  17.5 12.5 %all_gather.18 = bf16[384,512]{1,0:T(8,128)(2,1)S(1)} all-gather(bf16[384,128]{1,0:T(8,128)(2,1)} %param.26), channel_id=1, replica_groups=mesh['face'=8,'sub'=4] {'sub'}, dimensions={1}, use_global_device_ids=true | all-gather | bytes 491520 | tf_op jit(solution)/shard_map/all_gather | solution.py:61
  30.1 0.1 reshape.70
  30.1 13.3 %all-gather.1 = bf16[1,512,512]{2,1,0:T(8,128)(2,1)} all-gather(bf16[1,128,512]{2,1,0:T(8,128)(2,1)} %param.29), channel_id=3, replica_groups=mesh['face'=8,'sub'=4] {'sub'}, dimensions={1}, use_global_device_ids=true | all-gather | bytes 655360 | tf_op jit(solution)/shard_map/all_gather | solution.py:16
  43.5 10.7 %all-gather.3 = bf16[1,512,512]{2,1,0:T(8,128)(2,1)S(1)} all-gather(bf16[1,128,512]{2,1,0:T(8,128)(2,1)S(1)} %copy-done.3), channel_id=5, replica_groups=mesh['face'=8,'sub'=4] {'sub'}, dimensions={1}, use_global_device_ids=true | all-gather | bytes 655360 | tf_op jit(solution)/shard_map/all_gather | solution.py:16
  54.2 0.4 multiply_convert_fusion.4
  54.6 0.0 copy-start.1
  54.6 2.0 %gather_fusion.3 = bf16[512,512]{1,0:T(8,128)(2,1)S(1)} fusion(bf16[256,512]{1,0:T(8,128)(2,1)S(1)} %multiply_convert_fusion.4, s32[1024]{0:T(1024)S(1)} %pad_clamp_fusion.2), kind=kCustom, calls=%fused_computation.clone | custom fusion | bytes 1050624 | tf_op jit(solution)/shard_map/jit(_take)/gather | solution.py:71
  56.6 2.0 %gather_fusion.4 = bf16[512,512]{1,0:T(8,128)(2,1)S(1)} fusion(bf16[256,512]{1,0:T(8,128)(2,1)S(1)} %copy-done.1, s32[1024]{0:T(1024)S(1)} %pad_clamp_fusion.1), kind=kCustom, calls=%fused_computation.1.clone | custom fusion | bytes 1050624 | tf_op jit(solution)/shard_map/jit(_take)/gather | solution.py:71
  58.5 0.2 broadcast_select_fusion.2
  58.8 0.0 all-gather.8.cloned.1.call-done
  58.8 0.4 copy-done.6
  59.2 2.3 %constant_dynamic-update-slice_fusion.4 = (bf16[384,512]{1,0:T(8,128)(2,1)S(1)}, bf16[256,512]{1,0:T(8,128)(2,1)S(1)}) fusion(bf16[1024,512]{1,0:T(8,128)(2,1)} %all-gather.8.cloned.1.call-done, bf16[512,512]{1,0:T(8,128)(2,1)S(1)} %get-tuple-element.12, bf16[512,512]{1,0:T(8,128)(2,1)S(1)} %get-tuple-element.13, s32[512]{0:T(512)S(1)} %copy-done.6, ...), kind=kOutput, calls=%fused_computation.55 | convolution fusion | flops 675020800 | bytes 2885632 | tf_op jit(solution)/shard_map/dot_general | solution.py:76
  61.5 0.8 gather_fusion
  62.4 0.1 select_select_fusion
  62.5 0.6 slice_bitcast_fusion
  63.1 3.5 %collective-permute-start.1 = (bf16[32,512]{1,0:T(8,128)(2,1)}, bf16[32,512]{1,0:T(8,128)(2,1)}, u32[]{:S(2)}, u32[]{:S(2)}) collective-permute-start(bf16[32,512]{1,0:T(8,128)(2,1)} %get-tuple-element.6), channel_id=1, source_target_pairs={{0,28},{4,0},{8,4},{12,8},{16,12},{20,16},{24,20},{28,24},{1,29},{... | collective-permute-start | bytes 98312 | tf_op jit(solution)/shard_map/ppermute | solution.py:10
  66.7 0.4 collective-permute-start.2
  67.1 2.5 %collective-permute-start.3 = (bf16[32,512]{1,0:T(8,128)(2,1)}, bf16[32,512]{1,0:T(8,128)(2,1)S(1)}, u32[]{:S(2)}, u32[]{:S(2)}) collective-permute-start(bf16[32,512]{1,0:T(8,128)(2,1)} %get-tuple-element.4), channel_id=1, source_target_pairs={{0,3},{1,0},{2,1},{3,2},{4,7},{5,4},{6,5},{7,6},{8,11},{9,8},{10,9... | collective-permute-start | bytes 98312 | tf_op jit(solution)/shard_map/ppermute | solution.py:10
  69.6 7.5 %gather_fusion.2 = bf16[2048,512]{1,0:T(8,128)(2,1)S(1)} fusion(bf16[256,512]{1,0:T(8,128)(2,1)S(1)} %get-tuple-element.11, s32[2048]{0:T(1024)S(1)} %fusion.47), kind=kCustom, calls=%fused_computation.4 | custom fusion | bytes 4202496 | tf_op jit(solution)/shard_map/jit(_take)/gather | solution.py:91
  77.1 2.2 %broadcast_select_fusion = bf16[2048,512]{1,0:T(8,128)(2,1)} fusion(bf16[2048,512]{1,0:T(8,128)(2,1)S(1)} %gather_fusion.2, pred[2048]{0:T(1024)(128)(4,1)} %compare_and_fusion), kind=kLoop, calls=%fused_computation.14 | loop fusion | flops 1048576 | bytes 4196352 | tf_op jit(solution)/shard_map/jit(_take)/select_n | solution.py:91
  79.4 0.8 constant_dynamic-update-slice_fusion.3
  80.1 0.8 constant_dynamic-update-slice_fusion.2
  80.9 7.5 %gather_fusion.1 = bf16[2048,512]{1,0:T(8,128)(2,1)S(1)} fusion(bf16[384,512]{1,0:T(8,128)(2,1)S(1)} %constant_dynamic-update-slice_fusion, s32[2048]{0:T(1024)S(1)} %fusion.46), kind=kCustom, calls=%fused_computation.3 | custom fusion | bytes 4202496 | tf_op jit(solution)/shard_map/jit(_take)/gather | solution.py:94
  88.5 1.6 %broadcast_select_fusion.1 = bf16[2048,512]{1,0:T(8,128)(2,1)} fusion(bf16[2048,512]{1,0:T(8,128)(2,1)S(1)} %gather_fusion.1, pred[2048]{0:T(1024)(128)(4,1)S(1)} %copy-done.5), kind=kLoop, calls=%fused_computation.15 | loop fusion | flops 1048576 | bytes 4196352 | tf_op jit(solution)/shard_map/jit(_take)/select_n | solution.py:94
  90.0 8.5 %add_convert_fusion = bf16[2048,512]{1,0:T(8,128)(2,1)S(1)} fusion(bf16[2048,512]{1,0:T(8,128)(2,1)} %param.18, bf16[2048,512]{1,0:T(8,128)(2,1)} %broadcast_select_fusion, bf16[2048,512]{1,0:T(8,128)(2,1)} %broadcast_select_fusion.1, bf16[1,1536,512]{2,1,0:T(8,128)(2,1)} %all-gather.10.cloned.1.call-done, bf16[1,512,512]{2,1,0:T(8,128)(2,1)} %all-gather.1), kind=kOutput, calls=%fused_computation.11 | convolution fusion | flops 4322230272 | bytes 10485760 | tf_op jit(solution)/shard_map/dot_general | solution.py:14
  98.6 1.8 %fusion.8 = bf16[256,512]{1,0:T(8,128)(2,1)} fusion(bf16[2048,512]{1,0:T(8,128)(2,1)S(1)} %add_convert_fusion, s32[2048]{0:T(1024)S(1)} %copy-done.4), kind=kOutput, calls=%fused_computation.20 | convolution fusion | flops 537526272 | bytes 2367488 | tf_op jit(solution)/shard_map/dot_general | solution.py:101
  100.4 4.8 %all-gather.12.cloned.1.call-done = bf16[1,1024,512]{2,1,0:T(8,128)(2,1)} async-done(((bf16[1,256,512]{2,1,0:T(8,128)(2,1)}), bf16[1,1024,512]{2,1,0:T(8,128)(2,1)}) %all-gather.12.cloned.1.call-update) | async-done | bytes 1048592 | tf_op jit(solution)/shard_map/all_gather | solution.py:16
  105.3 2.0 %fusion.10 = bf16[256,512]{1,0:T(8,128)(2,1)S(1)} fusion(bf16[1,512,512]{2,1,0:T(8,128)(2,1)S(1)} %all-gather.3, bf16[1,1024,512]{2,1,0:T(8,128)(2,1)} %all-gather.12.cloned.1.call-done, bf16[256,512]{1,0:T(8,128)(2,1)} %fusion.8, bf16[256,512]{1,0:T(8,128)(2,1)S(1)} %get-tuple-element.11), kind=kOutput, calls=%fused_computation.22 | convolution fusion | flops 404750336 | bytes 2359296 | tf_op jit(solution)/shard_map/dot_general | solution.py:14
  107.3 0.2 fusion.59
  107.5 39.2 %psum.7 = f32[1,512]{1,0:T(1,128)S(1)} all-reduce(f32[1,512]{1,0:T(1,128)S(1)} %fusion.59), channel_id=1, replica_groups=mesh['face'=8,'sub'=4] {'face','sub'}, use_global_device_ids=true, to_apply=%region_0.2 | all-reduce | flops 512 | bytes 4096 | tf_op jit(solution)/shard_map/psum | solution.py:111
  146.8 0.6 broadcast_multiply_fusion
  (26 shorter events, 0.1 us)
Async XLA Ops:
  7.2 47.0 %copy-start = (bf16[256,384]{1,0:T(8,128)(2,1)S(1)}, bf16[256,384]{1,0:T(8,128)(2,1)}, u32[]{:S(2)}) copy-start(bf16[256,384]{1,0:T(8,128)(2,1)} %param.19) | copy-start | bytes 589828
  7.2 36.3 %copy-start.3 = (bf16[1,128,512]{2,1,0:T(8,128)(2,1)S(1)}, bf16[1,128,512]{2,1,0:T(8,128)(2,1)}, u32[]{:S(2)}) copy-start(bf16[1,128,512]{2,1,0:T(8,128)(2,1)} %param.31) | copy-start | bytes 393220
  7.2 51.6 %all-gather.8.cloned.1.call-start = ((), (), s32[]{:S(2)}) async-start(), calls=%async_computation | async-start | bytes 1310720 | tf_op jit(solution)/shard_map/all_gather | solution.py:16
  7.9 82.1 %all-gather.10.cloned.1.call-start = ((), (), s32[]{:S(2)}) async-start(), calls=%async_computation.1 | async-start | bytes 1966080 | tf_op jit(solution)/shard_map/all_gather | solution.py:25
  8.7 96.6 %all-gather.12.cloned.1.call-start = ((), (), s32[]{:S(2)}) async-start(), calls=%async_computation.2 | async-start | bytes 1310720 | tf_op jit(solution)/shard_map/all_gather | solution.py:16
  54.6 2.0 %copy-start.1 = (bf16[256,512]{1,0:T(8,128)(2,1)S(1)}, bf16[256,512]{1,0:T(8,128)(2,1)}, u32[]{:S(2)}) copy-start(bf16[256,512]{1,0:T(8,128)(2,1)} %param.17) | copy-start | bytes 786436
  58.5 0.7 copy-start.6
  63.1 16.2 %collective-permute-start = (bf16[32,512]{1,0:T(8,128)(2,1)}, bf16[32,512]{1,0:T(8,128)(2,1)}, u32[]{:S(2)}, u32[]{:S(2)}) collective-permute-start(bf16[32,512]{1,0:T(8,128)(2,1)} %get-tuple-element.7), channel_id=1, source_target_pairs={{0,4},{4,8},{8,12},{12,16},{16,20},{20,24},{24,28},{28,0},{1,5},{5... | collective-permute-start | bytes 98312 | tf_op jit(solution)/shard_map/ppermute | solution.py:10
  63.1 17.0 %collective-permute-start.1 = (bf16[32,512]{1,0:T(8,128)(2,1)}, bf16[32,512]{1,0:T(8,128)(2,1)}, u32[]{:S(2)}, u32[]{:S(2)}) collective-permute-start(bf16[32,512]{1,0:T(8,128)(2,1)} %get-tuple-element.6), channel_id=1, source_target_pairs={{0,28},{4,0},{8,4},{12,8},{16,12},{20,16},{24,20},{28,24},{1,29},{... | collective-permute-start | bytes 98312 | tf_op jit(solution)/shard_map/ppermute | solution.py:10
  66.7 14.2 %collective-permute-start.2 = (bf16[32,512]{1,0:T(8,128)(2,1)}, bf16[32,512]{1,0:T(8,128)(2,1)S(1)}, u32[]{:S(2)}, u32[]{:S(2)}) collective-permute-start(bf16[32,512]{1,0:T(8,128)(2,1)} %get-tuple-element.5), channel_id=1, source_target_pairs={{0,1},{1,2},{2,3},{3,0},{4,5},{5,6},{6,7},{7,4},{8,9},{9,10},{10,1... | collective-permute-start | bytes 98312 | tf_op jit(solution)/shard_map/ppermute | solution.py:10
  67.1 13.8 %collective-permute-start.3 = (bf16[32,512]{1,0:T(8,128)(2,1)}, bf16[32,512]{1,0:T(8,128)(2,1)S(1)}, u32[]{:S(2)}, u32[]{:S(2)}) collective-permute-start(bf16[32,512]{1,0:T(8,128)(2,1)} %get-tuple-element.4), channel_id=1, source_target_pairs={{0,3},{1,0},{2,1},{3,2},{4,7},{5,4},{6,5},{7,6},{8,11},{9,8},{10,9... | collective-permute-start | bytes 98312 | tf_op jit(solution)/shard_map/ppermute | solution.py:10
  80.9 7.6 %copy-start.5 = (pred[2048]{0:T(1024)(128)(4,1)S(1)}, pred[2048]{0:T(1024)(128)(4,1)}, u32[]{:S(2)}) copy-start(pred[2048]{0:T(1024)(128)(4,1)} %compare_and_fusion.1) | copy-start | bytes 6148
  90.0 8.5 %copy-start.4 = (s32[2048]{0:T(1024)S(1)}, s32[2048]{0:T(1024)}, u32[]{:S(2)}) copy-start(s32[2048]{0:T(1024)} %param.21) | copy-start | bytes 24580
  98.6 8.7 %copy-start.8 = (bf16[2048,512]{1,0:T(8,128)(2,1)}, bf16[2048,512]{1,0:T(8,128)(2,1)S(1)}, u32[]{:S(2)}) copy-start(bf16[2048,512]{1,0:T(8,128)(2,1)S(1)} %add_convert_fusion) | copy-start | bytes 6291460
  100.4 6.9 %copy-start.7 = (f32[256]{0:T(256)S(1)}, f32[256]{0:T(256)}, u32[]{:S(2)}) copy-start(f32[256]{0:T(256)} %param.25) | copy-start | bytes 3076
  107.3 40.1 %copy-start.2 = (bf16[256,512]{1,0:T(8,128)(2,1)}, bf16[256,512]{1,0:T(8,128)(2,1)S(1)}, u32[]{:S(2)}) copy-start(bf16[256,512]{1,0:T(8,128)(2,1)S(1)} %fusion.10) | copy-start | bytes 786436
Sparse Core Ops, SparseCore 0:
  9.8 32.7 all-gather.7
  44.4 32.7 all-gather.9
  79.1 26.1 all-gather.11
where the time goes:
time: 155 us; the launch traced here: 154 us
  blocking collectives  75.8 us (49%)
  local copies, waits for them, and re-layouts  22.6 us (15%)
  matrix products  15.3 us (10%)
  between operations  14 us (9%)
  other arithmetic  12.7 us (8%)
  waiting for transfers between devices  6.92 us (4%)
  starting transfers between devices  6.58 us (4%)
    psum x1, blocking collectives, per_device(): stacked = lax.psum(jnp.stack(totals), ('face', 'sub'))  39.2 us
    all_gather x2, blocking collectives, fold_rows(): lax.all_gather(weight, 'sub', axis=0, tiled=True)  24 us
    all_gather x1, blocking collectives, per_device(): lax.all_gather(grid_weight, 'sub', axis=1, tiled=True)  12.5 us
    dot_general x2, matrix products, fold_rows(): jnp.dot(operand, lax.all_gather(weight, 'sub', axis=0, tiled=True), prefe...  10.5 us
    gather x1, local copies, waits for them, and re-layouts, per_device(): jnp.take(node_table, senders, axis=0)  7.54 us
    gather x1, local copies, waits for them, and re-layouts, per_device(): receiving_rows = jnp.take(latent, receivers, axis=0)  7.53 us
    ppermute x4, starting transfers between devices, passed_along(): return lax.ppermute(value, axis, pairs)  6.47 us
    all_gather x2, waiting for transfers between devices, fold_rows(): lax.all_gather(weight, 'sub', axis=0, tiled=True)  4.85 us
  transfers between devices with their start and end apart: 7, of which 1 were waited for; matrix products, arithmetic and copies ran while one was open for 31% of the time, Pallas kernels for 0%

commit v1 on v0

--- a/solution.py
+++ b/solution.py
@@ -108,7 +108,7 @@
         jnp.bfloat16
     )
     totals = [jnp.dot(node_area, latent.astype(jnp.float32), precision=lax.Precision.HIGHEST)]
-    stacked = lax.psum(jnp.stack(totals), ("face", "sub"))
+    stacked = jnp.sum(lax.all_gather(jnp.stack(totals), ("face", "sub")), axis=0)
     masses = stacked / nodes_all
     return (latent, edge_state, masses)
 

time: 155 us -> 183 us (1.18)
  blocking collectives: 75.8 us -> 104 us
    all_gather x0 -> x1, blocking collectives: none -> 67.1 us  [per_device(): lax.all_gather(jnp.stack(totals), ('face', 'sub'))]
    psum x1 -> x0, blocking collectives: 39.2 us -> none  [per_device(): stacked = lax.psum(jnp.stack(totals), ('face', 'sub'))]
  transfers between devices with their start and end apart: 7 -> 7, of which waited for: 1 -> 1; matrix products, arithmetic and copies ran while one was open for 31% -> 26% of each run, Pallas kernels for 0% -> 0%
where the time goes in v1:
time: 183 us; the launch traced here: 182 us
  blocking collectives  104 us (57%)
  local copies, waits for them, and re-layouts  22.6 us (12%)
  matrix products  15.3 us (8%)
  between operations  14 us (8%)
  other arithmetic  12.8 us (7%)
  waiting for transfers between devices  6.92 us (4%)
  starting transfers between devices  6.58 us (4%)
    all_gather x1, blocking collectives, per_device(): lax.all_gather(jnp.stack(totals), ('face', 'sub'))  67.1 us
    all_gather x2, blocking collectives, fold_rows(): lax.all_gather(weight, 'sub', axis=0, tiled=True)  24 us
    all_gather x1, blocking collectives, per_device(): lax.all_gather(grid_weight, 'sub', axis=1, tiled=True)  12.5 us
    dot_general x2, matrix products, fold_rows(): jnp.dot(operand, lax.all_gather(weight, 'sub', axis=0, tiled=True), prefe...  10.5 us
    gather x1, local copies, waits for them, and re-layouts, per_device(): jnp.take(node_table, senders, axis=0)  7.54 us
    gather x1, local copies, waits for them, and re-layouts, per_device(): receiving_rows = jnp.take(latent, receivers, axis=0)  7.53 us
    ppermute x4, starting transfers between devices, passed_along(): return lax.ppermute(value, axis, pairs)  6.47 us
    all_gather x2, waiting for transfers between devices, fold_rows(): lax.all_gather(weight, 'sub', axis=0, tiled=True)  4.85 us
  transfers between devices with their start and end apart: 7, of which 1 were waited for; matrix products, arithmetic and copies ran while one was open for 26% of the time, Pallas kernels for 0%

profile of v1, /device:TPU:0, one launch (start us, length us, event | category | flops | bytes accessed | tf_op | source)
XLA Modules:
  0.0 181.8 jit_solution(9777850057149666593)
XLA Ops:
  7.2 0.0 copy-start
  7.2 0.0 all-gather.10.cloned.1.call-start
  7.2 0.7 all-gather.10.cloned.1.call-update
  7.9 0.0 all-gather.12.cloned.1.call-start
  8.0 0.7 all-gather.12.cloned.1.call-update
  8.7 0.0 all-gather.14.cloned.1.call-start
  8.7 0.7 all-gather.14.cloned.1.call-update
  9.4 0.7 compare_select_fusion.2
  10.1 0.7 compare_and_fusion.2
  10.8 0.7 compare_select_fusion.3
  11.5 0.7 compare_and_fusion.3
  12.2 0.7 broadcast_maximum_fusion
  12.8 0.7 compare_bitcast_fusion.1
  13.5 0.7 fusion.46
  14.2 1.3 compare_and_fusion.1
  15.5 0.7 fusion.47
  16.2 1.3 compare_and_fusion
  17.5 12.5 %all_gather.21 = bf16[384,512]{1,0:T(8,128)(2,1)S(1)} all-gather(bf16[384,128]{1,0:T(8,128)(2,1)} %param.26), channel_id=1, replica_groups=mesh['face'=8,'sub'=4] {'sub'}, dimensions={1}, use_global_device_ids=true | all-gather | bytes 491520 | tf_op jit(solution)/shard_map/all_gather | solution.py:61
  30.1 0.1 reshape.81
  30.1 13.3 %all-gather.1 = bf16[1,512,512]{2,1,0:T(8,128)(2,1)} all-gather(bf16[1,128,512]{2,1,0:T(8,128)(2,1)} %param.29), channel_id=3, replica_groups=mesh['face'=8,'sub'=4] {'sub'}, dimensions={1}, use_global_device_ids=true | all-gather | bytes 655360 | tf_op jit(solution)/shard_map/all_gather | solution.py:16
  43.5 10.7 %all-gather.3 = bf16[1,512,512]{2,1,0:T(8,128)(2,1)S(1)} all-gather(bf16[1,128,512]{2,1,0:T(8,128)(2,1)S(1)} %copy-done.3), channel_id=5, replica_groups=mesh['face'=8,'sub'=4] {'sub'}, dimensions={1}, use_global_device_ids=true | all-gather | bytes 655360 | tf_op jit(solution)/shard_map/all_gather | solution.py:16
  54.2 0.4 multiply_convert_fusion.4
  54.6 2.0 %gather_fusion.3 = bf16[512,512]{1,0:T(8,128)(2,1)S(1)} fusion(bf16[256,512]{1,0:T(8,128)(2,1)S(1)} %multiply_convert_fusion.4, s32[1024]{0:T(1024)S(1)} %pad_clamp_fusion.2), kind=kCustom, calls=%fused_computation.clone | custom fusion | bytes 1050624 | tf_op jit(solution)/shard_map/jit(_take)/gather | solution.py:71
  56.6 2.0 %gather_fusion.4 = bf16[512,512]{1,0:T(8,128)(2,1)S(1)} fusion(bf16[256,512]{1,0:T(8,128)(2,1)S(1)} %copy-done.1, s32[1024]{0:T(1024)S(1)} %pad_clamp_fusion.1), kind=kCustom, calls=%fused_computation.1.clone | custom fusion | bytes 1050624 | tf_op jit(solution)/shard_map/jit(_take)/gather | solution.py:71
  58.5 0.2 broadcast_select_fusion.2
  58.8 0.0 all-gather.10.cloned.1.call-done
  58.8 0.4 copy-done.6
  59.2 2.3 %constant_dynamic-update-slice_fusion.4 = (bf16[384,512]{1,0:T(8,128)(2,1)S(1)}, bf16[256,512]{1,0:T(8,128)(2,1)S(1)}) fusion(bf16[1024,512]{1,0:T(8,128)(2,1)} %all-gather.10.cloned.1.call-done, bf16[512,512]{1,0:T(8,128)(2,1)S(1)} %get-tuple-element.12, bf16[512,512]{1,0:T(8,128)(2,1)S(1)} %get-tuple-element.13, s32[512]{0:T(512)S(1)} %copy-done.6, ...), kind=kOutput, calls=%fused_computation.56 | convolution fusion | flops 675020800 | bytes 2885632 | tf_op jit(solution)/shard_map/dot_general | solution.py:76
  61.5 0.8 gather_fusion
  62.4 0.1 select_select_fusion
  62.5 0.6 slice_bitcast_fusion
  63.1 3.5 %collective-permute-start.1 = (bf16[32,512]{1,0:T(8,128)(2,1)}, bf16[32,512]{1,0:T(8,128)(2,1)}, u32[]{:S(2)}, u32[]{:S(2)}) collective-permute-start(bf16[32,512]{1,0:T(8,128)(2,1)} %get-tuple-element.6), channel_id=1, source_target_pairs={{0,28},{4,0},{8,4},{12,8},{16,12},{20,16},{24,20},{28,24},{1,29},{... | collective-permute-start | bytes 98312 | tf_op jit(solution)/shard_map/ppermute | solution.py:10
  66.7 0.4 collective-permute-start.2
  67.1 2.5 %collective-permute-start.3 = (bf16[32,512]{1,0:T(8,128)(2,1)}, bf16[32,512]{1,0:T(8,128)(2,1)S(1)}, u32[]{:S(2)}, u32[]{:S(2)}) collective-permute-start(bf16[32,512]{1,0:T(8,128)(2,1)} %get-tuple-element.4), channel_id=1, source_target_pairs={{0,3},{1,0},{2,1},{3,2},{4,7},{5,4},{6,5},{7,6},{8,11},{9,8},{10,9... | collective-permute-start | bytes 98312 | tf_op jit(solution)/shard_map/ppermute | solution.py:10
  69.6 7.5 %gather_fusion.2 = bf16[2048,512]{1,0:T(8,128)(2,1)S(1)} fusion(bf16[256,512]{1,0:T(8,128)(2,1)S(1)} %get-tuple-element.11, s32[2048]{0:T(1024)S(1)} %fusion.47), kind=kCustom, calls=%fused_computation.4 | custom fusion | bytes 4202496 | tf_op jit(solution)/shard_map/jit(_take)/gather | solution.py:91
  77.1 2.2 %broadcast_select_fusion = bf16[2048,512]{1,0:T(8,128)(2,1)} fusion(bf16[2048,512]{1,0:T(8,128)(2,1)S(1)} %gather_fusion.2, pred[2048]{0:T(1024)(128)(4,1)} %compare_and_fusion), kind=kLoop, calls=%fused_computation.14 | loop fusion | flops 1048576 | bytes 4196352 | tf_op jit(solution)/shard_map/jit(_take)/select_n | solution.py:91
  79.4 0.8 constant_dynamic-update-slice_fusion.3
  80.1 0.8 constant_dynamic-update-slice_fusion.2
  80.9 7.5 %gather_fusion.1 = bf16[2048,512]{1,0:T(8,128)(2,1)S(1)} fusion(bf16[384,512]{1,0:T(8,128)(2,1)S(1)} %constant_dynamic-update-slice_fusion, s32[2048]{0:T(1024)S(1)} %fusion.46), kind=kCustom, calls=%fused_computation.3 | custom fusion | bytes 4202496 | tf_op jit(solution)/shard_map/jit(_take)/gather | solution.py:94
  88.5 1.6 broadcast_select_fusion.1
  90.0 8.5 %add_convert_fusion = bf16[2048,512]{1,0:T(8,128)(2,1)S(1)} fusion(bf16[2048,512]{1,0:T(8,128)(2,1)} %param.18, bf16[2048,512]{1,0:T(8,128)(2,1)} %broadcast_select_fusion, bf16[2048,512]{1,0:T(8,128)(2,1)} %broadcast_select_fusion.1, bf16[1,1536,512]{2,1,0:T(8,128)(2,1)} %all-gather.12.cloned.1.call-done, bf16[1,512,512]{2,1,0:T(8,128)(2,1)} %all-gather.1), kind=kOutput, calls=%fused_computation.11 | convolution fusion | flops 4322230272 | bytes 10485760 | tf_op jit(solution)/shard_map/dot_general | solution.py:14
  98.6 1.8 %fusion.8 = bf16[256,512]{1,0:T(8,128)(2,1)} fusion(bf16[2048,512]{1,0:T(8,128)(2,1)S(1)} %add_convert_fusion, s32[2048]{0:T(1024)S(1)} %copy-done.4), kind=kOutput, calls=%fused_computation.20 | convolution fusion | flops 537526272 | bytes 2367488 | tf_op jit(solution)/shard_map/dot_general | solution.py:101
  100.4 4.8 %all-gather.14.cloned.1.call-done = bf16[1,1024,512]{2,1,0:T(8,128)(2,1)} async-done(((bf16[1,256,512]{2,1,0:T(8,128)(2,1)}), bf16[1,1024,512]{2,1,0:T(8,128)(2,1)}) %all-gather.14.cloned.1.call-update) | async-done | bytes 1048592 | tf_op jit(solution)/shard_map/all_gather | solution.py:16
  105.3 2.0 %fusion.10 = bf16[256,512]{1,0:T(8,128)(2,1)S(1)} fusion(bf16[1,512,512]{2,1,0:T(8,128)(2,1)S(1)} %all-gather.3, bf16[1,1024,512]{2,1,0:T(8,128)(2,1)} %all-gather.14.cloned.1.call-done, bf16[256,512]{1,0:T(8,128)(2,1)} %fusion.8, bf16[256,512]{1,0:T(8,128)(2,1)S(1)} %get-tuple-element.11), kind=kOutput, calls=%fused_computation.22 | convolution fusion | flops 404750336 | bytes 2359296 | tf_op jit(solution)/shard_map/dot_general | solution.py:14
  107.3 0.2 convolution_bitcast_fusion
  107.5 67.1 %all-gather.5 = f32[32,1,512]{2,1,0:T(1,128)S(1)} all-gather(f32[1,1,512]{2,1,0:T(1,128)S(1)} %convolution_bitcast_fusion), channel_id=6, replica_groups=mesh['face'=8,'sub'=4] {'face','sub'}, dimensions={0}, use_global_device_ids=true | all-gather | bytes 67584 | tf_op jit(solution)/shard_map/all_gather | solution.py:111
  174.6 0.1 reduce.1
  174.7 0.6 broadcast_multiply_fusion
  (27 shorter events, 0.1 us)
Async XLA Ops:
  7.2 47.0 %copy-start = (bf16[256,384]{1,0:T(8,128)(2,1)S(1)}, bf16[256,384]{1,0:T(8,128)(2,1)}, u32[]{:S(2)}) copy-start(bf16[256,384]{1,0:T(8,128)(2,1)} %param.19) | copy-start | bytes 589828
  7.2 36.3 %copy-start.3 = (bf16[1,128,512]{2,1,0:T(8,128)(2,1)S(1)}, bf16[1,128,512]{2,1,0:T(8,128)(2,1)}, u32[]{:S(2)}) copy-start(bf16[1,128,512]{2,1,0:T(8,128)(2,1)} %param.31) | copy-start | bytes 393220
  7.2 51.6 %all-gather.10.cloned.1.call-start = ((), (), s32[]{:S(2)}) async-start(), calls=%async_computation | async-start | bytes 1310720 | tf_op jit(solution)/shard_map/all_gather | solution.py:16
  7.9 82.1 %all-gather.12.cloned.1.call-start = ((), (), s32[]{:S(2)}) async-start(), calls=%async_computation.1 | async-start | bytes 1966080 | tf_op jit(solution)/shard_map/all_gather | solution.py:25
  8.7 96.6 %all-gather.14.cloned.1.call-start = ((), (), s32[]{:S(2)}) async-start(), calls=%async_computation.2 | async-start | bytes 1310720 | tf_op jit(solution)/shard_map/all_gather | solution.py:16
  54.6 2.0 %copy-start.1 = (bf16[256,512]{1,0:T(8,128)(2,1)S(1)}, bf16[256,512]{1,0:T(8,128)(2,1)}, u32[]{:S(2)}) copy-start(bf16[256,512]{1,0:T(8,128)(2,1)} %param.17) | copy-start | bytes 786436
  58.5 0.7 copy-start.6
  63.1 16.2 %collective-permute-start = (bf16[32,512]{1,0:T(8,128)(2,1)}, bf16[32,512]{1,0:T(8,128)(2,1)}, u32[]{:S(2)}, u32[]{:S(2)}) collective-permute-start(bf16[32,512]{1,0:T(8,128)(2,1)} %get-tuple-element.7), channel_id=1, source_target_pairs={{0,4},{4,8},{8,12},{12,16},{16,20},{20,24},{24,28},{28,0},{1,5},{5... | collective-permute-start | bytes 98312 | tf_op jit(solution)/shard_map/ppermute | solution.py:10
  63.1 17.0 %collective-permute-start.1 = (bf16[32,512]{1,0:T(8,128)(2,1)}, bf16[32,512]{1,0:T(8,128)(2,1)}, u32[]{:S(2)}, u32[]{:S(2)}) collective-permute-start(bf16[32,512]{1,0:T(8,128)(2,1)} %get-tuple-element.6), channel_id=1, source_target_pairs={{0,28},{4,0},{8,4},{12,8},{16,12},{20,16},{24,20},{28,24},{1,29},{... | collective-permute-start | bytes 98312 | tf_op jit(solution)/shard_map/ppermute | solution.py:10
  66.7 14.2 %collective-permute-start.2 = (bf16[32,512]{1,0:T(8,128)(2,1)}, bf16[32,512]{1,0:T(8,128)(2,1)S(1)}, u32[]{:S(2)}, u32[]{:S(2)}) collective-permute-start(bf16[32,512]{1,0:T(8,128)(2,1)} %get-tuple-element.5), channel_id=1, source_target_pairs={{0,1},{1,2},{2,3},{3,0},{4,5},{5,6},{6,7},{7,4},{8,9},{9,10},{10,1... | collective-permute-start | bytes 98312 | tf_op jit(solution)/shard_map/ppermute | solution.py:10
  67.1 13.8 %collective-permute-start.3 = (bf16[32,512]{1,0:T(8,128)(2,1)}, bf16[32,512]{1,0:T(8,128)(2,1)S(1)}, u32[]{:S(2)}, u32[]{:S(2)}) collective-permute-start(bf16[32,512]{1,0:T(8,128)(2,1)} %get-tuple-element.4), channel_id=1, source_target_pairs={{0,3},{1,0},{2,1},{3,2},{4,7},{5,4},{6,5},{7,6},{8,11},{9,8},{10,9... | collective-permute-start | bytes 98312 | tf_op jit(solution)/shard_map/ppermute | solution.py:10
  80.9 7.6 %copy-start.5 = (pred[2048]{0:T(1024)(128)(4,1)S(1)}, pred[2048]{0:T(1024)(128)(4,1)}, u32[]{:S(2)}) copy-start(pred[2048]{0:T(1024)(128)(4,1)} %compare_and_fusion.1) | copy-start | bytes 6148
  90.0 8.5 %copy-start.4 = (s32[2048]{0:T(1024)S(1)}, s32[2048]{0:T(1024)}, u32[]{:S(2)}) copy-start(s32[2048]{0:T(1024)} %param.21) | copy-start | bytes 24580
  98.6 8.7 %copy-start.8 = (bf16[2048,512]{1,0:T(8,128)(2,1)}, bf16[2048,512]{1,0:T(8,128)(2,1)S(1)}, u32[]{:S(2)}) copy-start(bf16[2048,512]{1,0:T(8,128)(2,1)S(1)} %add_convert_fusion) | copy-start | bytes 6291460
  100.4 6.9 %copy-start.7 = (f32[256]{0:T(256)S(1)}, f32[256]{0:T(256)}, u32[]{:S(2)}) copy-start(f32[256]{0:T(256)} %param.25) | copy-start | bytes 3076
  107.3 68.0 %copy-start.2 = (bf16[256,512]{1,0:T(8,128)(2,1)}, bf16[256,512]{1,0:T(8,128)(2,1)S(1)}, u32[]{:S(2)}) copy-start(bf16[256,512]{1,0:T(8,128)(2,1)S(1)} %fusion.10) | copy-start | bytes 786436
Sparse Core Ops, SparseCore 0:
  9.8 32.7 all-gather.9
  44.4 32.7 all-gather.11
  79.1 26.1 all-gather.13
